TPU v7x, 512 devices: a whole 4x8x8 slice. The times are simulated.
512 devices in a mesh: seq: 128 (over z, y, core), batch: 4 (over x).
Axes of the slice: x: 4, y: 8, z: 8, core: 2. Of those that a mesh axis runs over, the one named last changes fastest.
Arguments:
- tokens: bfloat16 [4, 131072, 1024], P('batch', 'seq'), may hold values from -24 to 24
- logits: bfloat16 [4, 131072, 256], P('batch', 'seq'), may hold values from -160 to 160
- slot_grad: bfloat16 [4, 256, 1024], P('batch', 'seq'), may hold values from -6 to 6
- phi_param: bfloat16 [1024, 256], P('seq'), may hold values from -0.1875 to 0.1875
Outputs:
- token_grad: bfloat16 [4, 131072, 1024], P('batch', 'seq')
- phi_grad: float32 [1024, 256], P('seq')
All inputs are finite; a program needn't handle non-finite values.
Results may differ from a plain program's by a relative error of at most 0.0049.
Values may be sent and summed in bfloat16 or wider, within the bound.
A program may use at most 64 MiB of HBM per device.

v0:
```python
import jax
import jax.numpy as jnp
from jax import lax
from jax.sharding import Mesh
from jax.sharding import PartitionSpec as P

SEQ = ("seq_0", "seq_1", "seq_2")


def laid_out(blocks, dim):
    blocks = jnp.moveaxis(blocks, 0, dim)
    shape = blocks.shape
    return blocks.reshape(*shape[:dim], shape[dim] * shape[dim + 1], *shape[dim + 2 :])


def gather_packed(arrays, axis, dims):
    vector = jnp.concatenate([a.reshape(-1) for a in arrays])
    lines, at, done = (lax.all_gather(vector, axis), 0, [])
    for a, dim in zip(arrays, dims):
        blocks = lines[:, at : at + a.size].reshape(-1, *a.shape)
        done.append(laid_out(blocks, dim))
        at += a.size
    return tuple(done)


def one_axis_at_a_time(shard, axes):
    for axis in axes:
        shard = lax.pmax(shard, axis)
    return shard


def over_axes(shard, axes):
    for axis in axes:
        shard = lax.psum(shard, axis)
    return shard


def own_block(blocks, axes, order):
    inside = blocks.shape[1:]
    blocks = blocks.reshape(*(lax.axis_size(a) for a in axes), *inside)
    blocks = jnp.moveaxis(blocks, order, range(len(axes))).reshape(-1, *inside)
    for k in order:
        blocks = lax.psum_scatter(blocks, axes[k], scatter_dimension=0, tiled=True)
    return blocks[0]


def split_up(shard, dim, length):
    before, after = (shard.shape[:dim], shard.shape[dim + 1 :])
    return jnp.moveaxis(shard.reshape(*before, length, -1, *after), dim, 0)


def sum_by_axis_2(shard, axes, order, dim):
    length = lax.axis_size(axes)
    return own_block(split_up(shard, dim, length), axes, order)


def sent_to_all(shard, axis):
    length = lax.axis_size(axis)
    return lax.all_to_all(
        jnp.broadcast_to(shard[None], (length, *shard.shape)), axis, 0, 0, tiled=True
    )


def over_copies(shard, axis):
    return sent_to_all(shard, axis).sum(axis=0)


def per_device(tokens, logits, slot_grad, phi_param):
    inputs = tokens[0]
    scores = logits[0].astype(jnp.float32)
    upstream, phi_full = gather_packed((slot_grad[0], phi_param), SEQ, (0, 0))
    weight_grad = lax.dot_general(
        inputs, upstream, (((1,), (1,)), ((), ())), preferred_element_type=jnp.float32
    )
    col_peak = one_axis_at_a_time(jnp.max(scores, axis=0, keepdims=True), SEQ)
    raw_weights = jnp.exp(scores - col_peak)
    col_total, weighted = (
        over_axes(jnp.sum(raw_weights, axis=0, keepdims=True), SEQ),
        over_axes(jnp.sum(raw_weights * weight_grad, axis=0, keepdims=True), SEQ),
    )
    dispatch = raw_weights / col_total
    col_dot = weighted / col_total
    logit_grad = (dispatch * (weight_grad - col_dot)).astype(jnp.bfloat16)
    dispatch_low = dispatch.astype(jnp.bfloat16)
    grad_scale = float(lax.axis_size(SEQ) * inputs.shape[0] // 16)
    token_sum = jnp.dot(dispatch_low, upstream, preferred_element_type=jnp.float32)
    token_sum = token_sum + lax.dot_general(
        logit_grad, phi_full, (((1,), (1,)), ((), ())), preferred_element_type=jnp.float32
    )
    token_grad = (grad_scale * token_sum).astype(jnp.bfloat16)[None]
    phi_terms = lax.dot_general(
        inputs, logit_grad, (((0,), (0,)), ((), ())), preferred_element_type=jnp.float32
    )
    phi_share = sum_by_axis_2(phi_terms, SEQ, (2, 0, 1), 0)
    phi_grad = over_copies(phi_share, "batch")
    return (token_grad, phi_grad)


def solution(mesh):
    finer = Mesh(
        mesh.devices.reshape(8, 8, 2, mesh.shape["batch"]), ("seq_0", "seq_1", "seq_2", "batch")
    )
    in_specs = (P("batch", SEQ, None), P("batch", SEQ, None), P("batch", SEQ, None), P(SEQ, None))
    out_specs = (P("batch", SEQ, None), P(SEQ, None))
    return jax.shard_map(
        per_device, mesh=finer, in_specs=in_specs, out_specs=out_specs, check_vma=False
    )
```

profile of v0, /device:TPU:2, one launch (start us, length us, event | category | flops | bytes accessed | tf_op | source)
XLA Modules:
  0.0 258.3 jit_solution(13024102402856939157)
XLA Ops:
  7.2 0.0 copy-start
  7.2 0.0 all-gather.3.cloned.1.call-start
  7.2 0.8 copy.17
  8.1 0.7 copy.19
  8.7 0.6 pad_maximum_fusion
  9.3 0.0 all-gather.3.cloned.1.call-update
  9.4 0.0 reduce-scatter.4.cloned.1.call-start
  9.4 2.1 copy.13
  11.5 1.2 reduce_max.16
  12.7 23.2 %pmax.21 = f32[1,256]{1,0:T(1,128)S(1)} all-reduce(f32[1,256]{1,0:T(1,128)S(1)} %bitcast.75), channel_id=1, replica_groups=mesh['seq_0'=8,'seq_1'=8,'seq_2'=2,'batch'=4] {'seq_0'}, use_global_device_ids=true, to_apply=%region_1.0 | all-reduce | flops 256 | bytes 2048 | tf_op jit(solution)/shard_map/pmax | solution.py:28
  35.9 17.6 %pmax.22 = f32[1,256]{1,0:T(1,128)S(1)} all-reduce(f32[1,256]{1,0:T(1,128)S(1)} %pmax.21), channel_id=1, replica_groups=mesh['seq_0'=8,'seq_1'=8,'seq_2'=2,'batch'=4] {'seq_1'}, use_global_device_ids=true, to_apply=%region_2.0 | all-reduce | flops 256 | bytes 2048 | tf_op jit(solution)/shard_map/pmax | solution.py:28
  53.5 2.5 pmax.23
  55.9 39.5 %all-gather.3.cloned.1.call-done = bf16[524288]{0:T(1024)(128)(2,1)} async-done(((bf16[4096]{0:T(1024)(128)(2,1)}), bf16[524288]{0:T(1024)(128)(2,1)}) %all-gather.3.cloned.1.call-update) | async-done | bytes 1048592 | tf_op jit(solution)/shard_map/all_gather | solution.py:18
  95.5 1.5 reshape.38
  97.0 1.0 fusion.29
  98.0 1.2 reshape_reshape.9
  99.3 0.0 copy-done
  99.3 0.0 copy-start.3
  99.3 0.0 copy-start.1
  99.3 3.0 %fusion.20 = (f32[256]{0:T(256)S(1)}, f32[256]{0:T(256)S(1)}, f32[1024,256]{0,1:T(8,128)}) fusion(bf16[1,1024,256]{1,2,0:T(8,128)(2,1)} %copy.13, f32[256]{0:T(256)S(1)} %pmax.23, bf16[256,1024]{1,0:T(8,128)(2,1)S(1)} %reshape_reshape.9, bf16[1,1024,1024]{2,1,0:T(8,128)(2,1)S(1)} %copy-done), kind=kOutput, calls=%fused_computation.19 | convolution fusion | flops 538181120 | bytes 4197376 | tf_op jit(solution)/shard_map/dot_general | solution.py:72
  102.3 0.0 copy-done.3
  102.3 16.1 %all-reduce.1 = (f32[1,256]{1,0:T(1,128)S(1)}, f32[1,256]{1,0:T(1,128)S(1)}) all-reduce(f32[1,256]{1,0:T(1,128)S(1)} %bitcast.74, f32[1,256]{1,0:T(1,128)S(1)} %bitcast.73), channel_id=1, replica_groups=mesh['seq_0'=8,'seq_1'=8,'seq_2'=2,'batch'=4] {'seq_0'}, use_global_device_ids=true, to_apply=%region_5.0 | all-reduce | flops 512 | bytes 4096 | tf_op jit(solution)/shard_map/psum | solution.py:34
  118.4 15.9 %all-reduce = (f32[1,256]{1,0:T(1,128)S(1)}, f32[1,256]{1,0:T(1,128)S(1)}) all-reduce(f32[1,256]{1,0:T(1,128)S(1)} %get-tuple-element.6, f32[1,256]{1,0:T(1,128)S(1)} %get-tuple-element.7), channel_id=1, replica_groups=mesh['seq_0'=8,'seq_1'=8,'seq_2'=2,'batch'=4] {'seq_1'}, use_global_device_ids=true, to_apply=%region_6.0 | all-reduce | flops 512 | bytes 4096 | tf_op jit(solution)/shard_map/psum | solution.py:34
  134.3 2.5 all-reduce.2
  136.8 0.0 copy-done.1
  136.8 3.1 %fusion.8 = f32[1024,256]{0,1:T(8,128)} fusion(bf16[1,1024,1024]{2,1,0:T(8,128)(2,1)S(1)} %copy-done, f32[1024,256]{0,1:T(8,128)} %get-tuple-element.12, bf16[1,1024,256]{1,2,0:T(8,128)(2,1)S(1)} %copy-done.1, f32[256]{0:T(256)S(1)} %bitcast.68, f32[256]{0:T(256)S(1)} %bitcast.65, f32[256]{0:T(256)S(1)} %pmax.23), kind=kOutput, calls=%fused_computation.7 | convolution fusion | flops 538443776 | bytes 4721664 | tf_op jit(solution)/shard_map/dot_general | solution.py:91
  139.8 1.6 copy.14
  141.4 1.1 copy.15
  142.5 0.0 reduce-scatter.4.cloned.1.call-update
  142.5 0.0 reduce-scatter.6.cloned.1.call-start
  142.6 12.4 %reduce-scatter.4.cloned.1.call-done = f32[64,8,256]{2,1,0:T(8,128)} async-done(((f32[128,8,256]{2,1,0:T(8,128)}), f32[64,8,256]{2,1,0:T(8,128)}) %reduce-scatter.4.cloned.1.call-update) | async-done | bytes 524304 | tf_op jit(solution)/shard_map/reduce_scatter | solution.py:43
  154.9 0.0 reduce-scatter.6.cloned.1.call-update
  155.0 0.0 reduce-scatter.8.cloned.1.call-start
  155.0 45.3 %reduce-scatter.6.cloned.1.call-done = f32[8,8,256]{2,1,0:T(8,128)} async-done(((f32[64,8,256]{2,1,0:T(8,128)}), f32[8,8,256]{2,1,0:T(8,128)}) %reduce-scatter.6.cloned.1.call-update) | async-done | bytes 65552 | tf_op jit(solution)/shard_map/reduce_scatter | solution.py:43
  200.3 0.0 reduce-scatter.8.cloned.1.call-update
  200.3 0.0 copy-start.2
  200.3 4.1 %fusion.23 = f32[1024,1024]{1,0:T(8,128)} fusion(bf16[256,1024]{1,0:T(8,128)(2,1)} %copy-done.3, bf16[1,1024,256]{1,2,0:T(8,128)(2,1)} %copy.13, f32[256]{0:T(256)S(1)} %bitcast.66, f32[256]{0:T(256)S(1)} %pmax.23), kind=kOutput, calls=%fused_computation.22 | convolution fusion | flops 537919488 | bytes 5244928 | tf_op jit(solution)/shard_map/dot_general | solution.py:86
  204.4 1.3 reshape_reshape.10
  205.7 34.5 %reduce-scatter.8.cloned.1.call-done = f32[1,8,256]{2,1,0:T(8,128)} async-done(((f32[8,8,256]{2,1,0:T(8,128)}), f32[1,8,256]{2,1,0:T(8,128)}) %reduce-scatter.8.cloned.1.call-update) | async-done | bytes 8208 | tf_op jit(solution)/shard_map/reduce_scatter | solution.py:43
  240.2 1.3 broadcast_in_dim.21
  241.5 4.8 %all-to-all-start = ((f32[4,8,256]{2,1,0:T(8,128)}), f32[4,8,256]{2,1,0:T(8,128)S(1)}, u32[]{:S(2)}, u32[]{:S(2)}) async-start(f32[4,8,256]{2,1,0:T(8,128)} %broadcast_in_dim.21), calls=%async_computation.3 | async-start | bytes 65536 | tf_op jit(solution)/shard_map/all_to_all | solution.py:59
  246.3 0.0 copy-done.2
  246.3 4.9 %fusion.4 = bf16[1,1024,1024]{2,1,0:T(8,128)(2,1)} fusion(f32[1024,1024]{1,0:T(8,128)} %fusion.23, bf16[1024,256]{1,0:T(8,128)(2,1)S(1)} %reshape_reshape.10, f32[1024,256]{0,1:T(8,128)} %get-tuple-element.12, bf16[1,1024,256]{1,2,0:T(8,128)(2,1)S(1)} %copy-done.2, f32[256]{0:T(256)S(1)} %bitcast.69, f32[256]{0:T(256)S(1)} %bitcast.67, f32[256]{0:T(256)S(1)} %pmax.23), kind=kOutput, calls=%fused_computation.5 | convolution fusion | flops 541589504 | bytes 8391680 | tf_op jit(solution)/shard_map/dot_general | solution.py:87
  251.2 0.0 all-to-all-done
  251.2 0.6 reduce_sum.29
  (2 shorter events, 0.0 us)
Async XLA Ops:
  7.2 92.1 %copy-start = (bf16[1,1024,1024]{2,1,0:T(8,128)(2,1)S(1)}, bf16[1,1024,1024]{2,1,0:T(8,128)(2,1)}, u32[]{:S(2)}) copy-start(bf16[1,1024,1024]{2,1,0:T(8,128)(2,1)} %param.4) | copy-start | bytes 6291460
  7.2 88.3 %all-gather.3.cloned.1.call-start = ((), (), s32[]{:S(2)}) async-start(), calls=%async_computation.7 | async-start | bytes 1056768 | tf_op jit(solution)/shard_map/all_gather | solution.py:18
  9.4 145.6 %reduce-scatter.4.cloned.1.call-start = ((), (), s32[]{:S(2)}) async-start(), calls=%async_computation.4 | async-start | bytes 1572864 | tf_op jit(solution)/shard_map/reduce_scatter | solution.py:43
  99.3 3.0 %copy-start.3 = (bf16[256,1024]{1,0:T(8,128)(2,1)}, bf16[256,1024]{1,0:T(8,128)(2,1)S(1)}, u32[]{:S(2)}) copy-start(bf16[256,1024]{1,0:T(8,128)(2,1)S(1)} %reshape_reshape.9) | copy-start | bytes 1572868
  99.3 37.5 %copy-start.1 = (bf16[1,1024,256]{1,2,0:T(8,128)(2,1)S(1)}, bf16[1,1024,256]{1,2,0:T(8,128)(2,1)}, u32[]{:S(2)}) copy-start(bf16[1,1024,256]{1,2,0:T(8,128)(2,1)} %copy.13) | copy-start | bytes 1572868
  142.5 57.8 %reduce-scatter.6.cloned.1.call-start = ((), (), s32[]{:S(2)}) async-start(), calls=%async_computation.5 | async-start | bytes 589824 | tf_op jit(solution)/shard_map/reduce_scatter | solution.py:43
  155.0 85.3 %reduce-scatter.8.cloned.1.call-start = ((), (), s32[]{:S(2)}) async-start(), calls=%async_computation.6 | async-start | bytes 73728 | tf_op jit(solution)/shard_map/reduce_scatter | solution.py:43
  200.3 46.0 %copy-start.2 = (bf16[1,1024,256]{1,2,0:T(8,128)(2,1)S(1)}, bf16[1,1024,256]{1,2,0:T(8,128)(2,1)}, u32[]{:S(2)}) copy-start(bf16[1,1024,256]{1,2,0:T(8,128)(2,1)} %copy.13) | copy-start | bytes 1572868
  241.5 9.7 %all-to-all-start = ((f32[4,8,256]{2,1,0:T(8,128)}), f32[4,8,256]{2,1,0:T(8,128)S(1)}, u32[]{:S(2)}, u32[]{:S(2)}) async-start(f32[4,8,256]{2,1,0:T(8,128)} %broadcast_in_dim.21), calls=%async_computation.3 | async-start | bytes 65536 | tf_op jit(solution)/shard_map/all_to_all | solution.py:59
Sparse Core Ops, SparseCore 0:
  11.6 83.8 all-gather.2
  142.6 12.2 reduce-scatter.3
  157.7 42.5 reduce-scatter.5
  202.9 37.2 reduce-scatter.7
where the time goes:
time: 259 us; the launch traced here: 258 us
  waiting for transfers between devices  132 us (51%)
  blocking collectives  77.7 us (30%)
  matrix products  15 us (6%)
  between operations  13.8 us (5%)
  local copies, waits for them, and re-layouts  12.6 us (5%)
  starting transfers between devices  4.95 us (2%)
    reduce_scatter x3, waiting for transfers between devices, own_block(): blocks = lax.psum_scatter(blocks, axes[k], scatter_dimension=0, tiled=True)  92.2 us
    pmax x3, blocking collectives, one_axis_at_a_time(): shard = lax.pmax(shard, axis)  43.2 us
    all_gather x1, waiting for transfers between devices, gather_packed(): lines, at, done = (lax.all_gather(vector, axis), 0, [])  39.5 us
    psum x3, blocking collectives, over_axes(): shard = lax.psum(shard, axis)  34.5 us
  transfers between devices with their start and end apart: 5, of which 4 were waited for; matrix products, arithmetic and copies ran while one was open for 5% of the time, Pallas kernels for 0%

commit v1 on v0

v1 whole, which is shorter than its diff:
```python
import functools

import jax
import jax.numpy as jnp
from jax import lax
from jax.experimental import pallas as pl
from jax.experimental.pallas import tpu as pltpu
from jax.sharding import Mesh
from jax.sharding import PartitionSpec as P

SEQ = ("seq_0", "seq_1", "seq_2")
MESH = pl.DeviceIdType.MESH
F32 = jnp.float32
BF16 = jnp.bfloat16
NT = (((1,), (1,)), ((), ()))


def ring_order(n):
    return sorted(range(1, n), key=lambda k: (-min(k, n - k), k))


def kernel(
    sizes, tok_h, log_h, g_h, phi_h, tg_h, pg_o,
    tok, tokT, logv, gy, py, gall, pall, p, wg, st, sa, sb, dlow, lg,
    own, dsnd, drcv, zsnd, zrcv, ysnd, yrcv, xbuf, tgv,
    lsem, ssem, rsem, gsem, csem, osem,
):
    nz, ny, nc, nx = sizes
    z, y, c, x = (lax.axis_index(a) for a in (*SEQ, "batch"))
    ts, d = tok.shape
    slots = logv.shape[1]
    half = d // 2
    rank = y * nc + c
    n16 = ny * nc
    tile = min(256, ts)
    other = nc - 1 - c

    def row_peer(j):
        i = lax.rem(rank + j, n16)
        return (z, lax.div(i, nc), lax.rem(i, nc), x)

    def z_peer(k):
        return (lax.rem(z + k, nz), y, c, x)

    def y_peer(k):
        return (z, lax.rem(y + k, ny), c, x)

    def x_peer(k):
        return (z, y, c, lax.rem(x + k, nx))

    partner = (z, y, other, x)

    def send(src, dst, s, r, to):
        pltpu.make_async_remote_copy(
            src_ref=src, dst_ref=dst, send_sem=s, recv_sem=r, device_id=to, device_id_type=MESH
        ).start()

    def await_bytes(ref, sem):
        pltpu.make_async_copy(ref, ref, sem).wait()

    loads = [
        pltpu.make_async_copy(g_h, gy.at[rank], lsem.at[0]),
        pltpu.make_async_copy(phi_h, py.at[rank], lsem.at[1]),
        pltpu.make_async_copy(log_h, logv, lsem.at[2]),
        pltpu.make_async_copy(tok_h, tok, lsem.at[3]),
    ]
    for one in loads:
        one.start()

    barrier = pltpu.get_barrier_semaphore()
    peers = [row_peer(j) for j in range(1, n16)]
    peers += [z_peer(k) for k in range(1, nz)] + [x_peer(k) for k in range(1, nx)]
    for to in peers:
        pl.semaphore_signal(barrier, inc=1, device_id=to, device_id_type=MESH)
    loads[0].wait()
    loads[1].wait()
    pl.semaphore_wait(barrier, len(peers))

    for j in range(1, n16):
        send(gy.at[rank], gy.at[rank], ssem.at[0], rsem.at[0], row_peer(j))
    for j in range(1, n16):
        send(py.at[rank], py.at[rank], ssem.at[1], rsem.at[1], row_peer(j))

    loads[2].wait()
    scores = logv[...].astype(F32)
    peak = jnp.max(scores, axis=0, keepdims=True)
    raw = jnp.exp(scores - peak)
    p[...] = raw
    total = jnp.sum(raw, axis=0, keepdims=True)

    await_bytes(gy.at[pl.ds(0, n16 - 1)], rsem.at[0])
    block = jnp.concatenate([gy[i].astype(F32) for i in range(n16)], axis=0).astype(BF16)
    gall[0, z] = block[:, :half]
    gall[1, z] = block[:, half:]
    order = ring_order(nz)
    for k in order:
        send(gall.at[c, z], gall.at[c, z], ssem.at[2], gsem.at[k - 1], z_peer(k))

    loads[3].wait()
    dt = min(128, d)

    def turn(i, carry):
        r = pl.ds(pl.multiple_of(i * dt, dt), dt)
        tokT[r, :] = tok[:, r].T
        return carry

    lax.fori_loop(0, d // dt, turn, 0)

    for k in reversed(order):
        src = lax.rem(z + nz - k, nz)
        await_bytes(gall.at[c, src], gsem.at[k - 1])
        send(gall.at[c, src], gall.at[c, src], ssem.at[3], rsem.at[2], partner)
    await_bytes(gall.at[other, pl.ds(0, nz - 1)], rsem.at[2])

    g0 = gall[0].reshape(slots, half)
    g1 = gall[1].reshape(slots, half)

    def weigh(i, acc):
        r = pl.ds(pl.multiple_of(i * tile, tile), tile)
        t = tok[r, :]
        w = lax.dot_general(t[:, :half], g0, NT, preferred_element_type=F32)
        w = w + lax.dot_general(t[:, half:], g1, NT, preferred_element_type=F32)
        wg[r, :] = w
        return acc + jnp.sum(p[r, :] * w, axis=0, keepdims=True)

    dots = lax.fori_loop(0, ts // tile, weigh, jnp.zeros((1, slots), F32))

    def merged(parts):
        top = functools.reduce(jnp.maximum, [a[0:1] for a in parts])
        scale = [jnp.exp(a[0:1] - top) for a in parts]
        one = sum(a[1:2] * s for a, s in zip(parts, scale))
        two = sum(a[2:3] * s for a, s in zip(parts, scale))
        return jnp.concatenate([top, one, two, jnp.zeros_like(top)], axis=0)

    mine = jnp.concatenate([peak, total, dots, jnp.zeros_like(dots)], axis=0)
    st[0] = mine
    for k in order:
        send(st.at[0], sa.at[k - 1], ssem.at[4], rsem.at[3], z_peer(k))

    hb = n16 // 2
    await_bytes(py.at[pl.ds(0, n16 - 1)], rsem.at[1])
    pall[z] = py[...]
    for k in order:
        part = pl.ds(c * hb, hb)
        send(pall.at[z, part], pall.at[z, part], ssem.at[5], gsem.at[nz - 1 + k - 1], z_peer(k))

    await_bytes(sa, rsem.at[3])
    mine = merged([mine] + [sa[k] for k in range(nz - 1)])
    st[1] = mine
    for j in range(1, n16):
        send(st.at[1], sb.at[j - 1], ssem.at[6], rsem.at[4], row_peer(j))
    await_bytes(sb, rsem.at[4])
    mine = merged([mine] + [sb[k] for k in range(n16 - 1)])
    scale = jnp.exp(peak - mine[0:1]) / mine[1:2]
    center = mine[2:3] / mine[1:2]

    def grade(i, carry):
        r = pl.ds(pl.multiple_of(i * tile, tile), tile)
        dispatch = p[r, :] * scale
        dlow[r, :] = dispatch.astype(BF16)
        lg[r, :] = (dispatch * (wg[r, :] - center)).astype(BF16)
        return carry

    lax.fori_loop(0, ts // tile, grade, 0)

    rb = d // (nz * n16)
    zb = n16 * rb
    chunks = [*order, 0]
    for q, k in enumerate(chunks):
        to = lax.rem(z + k, nz)
        r = pl.ds(pl.multiple_of(to * zb, zb), zb)
        res = jnp.dot(tokT[r, :], lg[...], preferred_element_type=F32)
        res = res.reshape(ny, 2, rb, slots)
        keep = jnp.where(c == 0, res[:, 0], res[:, 1])
        give = jnp.where(c == 0, res[:, 1], res[:, 0])
        own[q] = keep.reshape(ny * rb, slots)
        dsnd[q] = give.reshape(ny * rb, slots).astype(BF16)
        send(dsnd.at[q], drcv.at[q], ssem.at[7], csem.at[q], partner)
    for q, k in enumerate(chunks):
        await_bytes(drcv.at[q], csem.at[q])
        both = own[q] + drcv[q].astype(F32)
        if k:
            zsnd[q] = both.astype(BF16)
            send(zsnd.at[q], zrcv.at[k - 1], ssem.at[8], rsem.at[5], z_peer(k))
        else:
            own[q] = both

    for k in reversed(order):
        src = lax.rem(z + nz - k, nz)
        part = pl.ds(c * hb, hb)
        await_bytes(pall.at[src, part], gsem.at[nz - 1 + k - 1])
        send(pall.at[src, part], pall.at[src, part], ssem.at[9], rsem.at[6], partner)
    await_bytes(pall.at[pl.ds(0, nz - 1), pl.ds(0, hb)], rsem.at[6])
    grad_scale = float(ts * nz * n16 // 16)

    def emit(i, carry):
        r = pl.ds(pl.multiple_of(i * tile, tile), tile)
        for h in range(2):
            g = gall[h].reshape(slots, half)
            ph = pall[h * nz // 2 : (h + 1) * nz // 2].astype(F32).reshape(half, slots).astype(BF16)
            s = jnp.dot(dlow[r, :], g, preferred_element_type=F32)
            s = s + lax.dot_general(lg[r, :], ph, NT, preferred_element_type=F32)
            tgv[r, h * half : (h + 1) * half] = (grad_scale * s).astype(BF16)
        pltpu.make_async_copy(tgv.at[r], tg_h.at[r], osem.at[i]).start()
        return carry

    lax.fori_loop(0, ts // tile, emit, 0)

    await_bytes(zrcv, rsem.at[5])
    acc = own[nz - 1]
    for k in range(nz - 1):
        acc = acc + zrcv[k].astype(F32)
    ysnd[...] = acc.reshape(ny, rb, slots)
    yorder = ring_order(ny)
    for k in yorder:
        send(ysnd.at[lax.rem(y + k, ny)], yrcv.at[k - 1], ssem.at[10], rsem.at[7], y_peer(k))
    acc = ysnd[y]
    await_bytes(yrcv, rsem.at[7])
    for k in range(ny - 1):
        acc = acc + yrcv[k]
    xbuf[x] = acc
    for k in ring_order(nx):
        send(xbuf.at[x], xbuf.at[x], ssem.at[11], rsem.at[8], x_peer(k))
    await_bytes(xbuf.at[pl.ds(0, nx - 1)], rsem.at[8])
    acc = xbuf[0]
    for k in range(1, nx):
        acc = acc + xbuf[k]
    pg_o[...] = acc

    await_bytes(gy.at[pl.ds(0, n16 - 1)], ssem.at[0])
    await_bytes(py.at[pl.ds(0, n16 - 1)], ssem.at[1])
    await_bytes(gall.at[0, pl.ds(0, nz - 1)], ssem.at[2])
    await_bytes(gall.at[0, pl.ds(0, nz - 1)], ssem.at[3])
    await_bytes(sa, ssem.at[4])
    await_bytes(pall.at[pl.ds(0, nz - 1), pl.ds(0, hb)], ssem.at[5])
    await_bytes(sb, ssem.at[6])
    await_bytes(drcv, ssem.at[7])
    await_bytes(zrcv, ssem.at[8])
    await_bytes(pall.at[pl.ds(0, nz - 1), pl.ds(0, hb)], ssem.at[9])
    await_bytes(yrcv, ssem.at[10])
    await_bytes(xbuf.at[pl.ds(0, nx - 1)], ssem.at[11])
    for i in range(ts // tile):
        r = pl.ds(i * tile, tile)
        pltpu.make_async_copy(tgv.at[r], tg_h.at[r], osem.at[i]).wait()


def per_device(sizes, tokens, logits, slot_grad, phi_param):
    nz, ny, nc, nx = sizes
    tokens, logits, slot_grad = tokens[0], logits[0], slot_grad[0]
    ts, d = tokens.shape
    slots = logits.shape[1]
    n16 = ny * nc
    rb = d // (nz * n16)
    sl = slots // (nz * n16)
    half = d // 2
    tile = min(256, ts)
    vm, dma = pltpu.VMEM, pltpu.SemaphoreType.DMA
    any_spec = pl.BlockSpec(memory_space=pl.ANY)
    scratch = [
        vm((ts, d), BF16), vm((d, ts), BF16), vm((ts, slots), BF16),
        vm((n16, sl, d), BF16), vm((n16, rb, slots), BF16),
        vm((2, nz, n16 * sl, half), BF16), vm((nz, n16, rb, slots), BF16),
        vm((ts, slots), F32), vm((ts, slots), F32),
        vm((2, 4, slots), F32), vm((nz - 1, 4, slots), F32), vm((n16 - 1, 4, slots), F32),
        vm((ts, slots), BF16), vm((ts, slots), BF16),
        vm((nz, ny * rb, slots), F32), vm((nz, ny * rb, slots), BF16), vm((nz, ny * rb, slots), BF16),
        vm((nz - 1, ny * rb, slots), BF16), vm((nz - 1, ny * rb, slots), BF16),
        vm((ny, rb, slots), F32), vm((ny - 1, rb, slots), F32),
        vm((nx, rb, slots), F32), vm((ts, d), BF16),
        dma((4,)), dma((12,)), dma((9,)), dma((2 * (nz - 1),)), dma((nz,)), dma((ts // tile,)),
    ]
    token_grad, phi_grad = pl.pallas_call(
        functools.partial(kernel, sizes),
        out_shape=(
            jax.ShapeDtypeStruct((ts, d), BF16),
            jax.ShapeDtypeStruct((rb, slots), F32),
        ),
        in_specs=[any_spec] * 4,
        out_specs=(any_spec, pl.BlockSpec(memory_space=pltpu.VMEM)),
        scratch_shapes=scratch,
        compiler_params=pltpu.CompilerParams(
            collective_id=0, has_side_effects=True, vmem_limit_bytes=48 * 1024 * 1024
        ),
        name="moe_dispatch_backward",
    )(tokens, logits, slot_grad, phi_param)
    return token_grad[None], phi_grad


def solution(mesh):
    shape = mesh.devices.shape
    nc = 2
    ny = 8 if shape[0] % 128 == 0 else 2
    sizes = (shape[0] // (ny * nc), ny, nc, shape[1])
    finer = Mesh(mesh.devices.reshape(sizes), (*SEQ, "batch"))
    in_specs = (P("batch", SEQ, None), P("batch", SEQ, None), P("batch", SEQ, None), P(SEQ, None))
    out_specs = (P("batch", SEQ, None), P(SEQ, None))
    return jax.shard_map(
        functools.partial(per_device, sizes),
        mesh=finer, in_specs=in_specs, out_specs=out_specs, check_vma=False,
    )
```

time: 259 us -> 66.1 us (0.26)
  the two profiles are of different devices: /device:TPU:2 before, /device:TPU:1 now
where the time goes in v1:
time: 66.1 us; the launch traced here: 65.3 us
  Pallas kernels  58.7 us (89%)
  local copies, waits for them, and re-layouts  5.92 us (9%)
    pallas_call x1, Pallas kernels, per_device(): pl.pallas_call(functools.partial(kernel, sizes), out_shape=(jax.ShapeDtyp...  58.7 us
    unnamed x10, local copies, waits for them, and re-layouts  5.92 us

profile of v1, /device:TPU:1, one launch (start us, length us, event | category | flops | bytes accessed | tf_op | source)
XLA Modules:
  0.0 65.3 jit_solution(17366246356215747281)
XLA Ops:
  0.6 0.0 copy-start
  0.6 1.6 %copy-done = bf16[1,1024,1024]{2,1,0:T(8,128)(2,1)S(1)} copy-done((bf16[1,1024,1024]{2,1,0:T(8,128)(2,1)S(1)}, bf16[1,1024,1024]{2,1,0:T(8,128)(2,1)}, u32[]{:S(2)}) %copy-start) | copy-done | bytes 2097176
  2.2 0.0 copy-start.1
  2.2 1.0 %copy-done.1 = bf16[1,1024,256]{2,1,0:T(8,128)(2,1)S(1)} copy-done((bf16[1,1024,256]{2,1,0:T(8,128)(2,1)S(1)}, bf16[1,1024,256]{2,1,0:T(8,128)(2,1)}, u32[]{:S(2)}) %copy-start.1) | copy-done | bytes 524312
  3.3 0.0 copy-start.2
  3.3 0.7 %copy-done.2 = bf16[1,2,1024]{2,1,0:T(2,128)(2,1)S(1)} copy-done((bf16[1,2,1024]{2,1,0:T(2,128)(2,1)S(1)}, bf16[1,2,1024]{2,1,0:T(2,128)(2,1)}, u32[]{:S(2)}) %copy-start.2) | copy-done | bytes 4120
  4.0 0.0 copy-start.3
  4.0 0.7 %copy-done.3 = bf16[8,256]{1,0:T(8,128)(2,1)S(1)} copy-done((bf16[8,256]{1,0:T(8,128)(2,1)S(1)}, bf16[8,256]{1,0:T(8,128)(2,1)}, u32[]{:S(2)}) %copy-start.3) | copy-done | bytes 4120
  4.6 58.7 %moe_dispatch_backward.1 = (bf16[1024,1024]{1,0:T(8,128)(2,1)S(1)}, f32[8,256]{1,0:T(8,128)S(1)}) custom-call(bf16[1024,1024]{1,0:T(8,128)(2,1)S(1)} %bitcast.4, bf16[1024,256]{1,0:T(8,128)(2,1)S(1)} %bitcast.6, bf16[2,1024]{1,0:T(2,128)(2,1)S(1)} %bitcast.7, bf16[8,256]{1,0:T(8,128)(2,1)S(1)} %copy-done.3), custom_call_target="tpu_custom_call" | custom-call | tf_op jit(solution)/shard_map/moe_dispatch_backward/pallas_call | solution.py:272
  63.4 1.3 %copy.8 = bf16[1,1024,1024]{2,1,0:T(8,128)(2,1)} copy(bf16[1,1024,1024]{2,1,0:T(8,128)(2,1)S(1)} %bitcast.5) | data formatting | bytes 4194304
  64.7 0.6 copy.9
Async XLA Ops:
  0.6 1.6 %copy-start = (bf16[1,1024,1024]{2,1,0:T(8,128)(2,1)S(1)}, bf16[1,1024,1024]{2,1,0:T(8,128)(2,1)}, u32[]{:S(2)}) copy-start(bf16[1,1024,1024]{2,1,0:T(8,128)(2,1)} %param.4) | copy-start | bytes 6291460
  2.2 1.0 %copy-start.1 = (bf16[1,1024,256]{2,1,0:T(8,128)(2,1)S(1)}, bf16[1,1024,256]{2,1,0:T(8,128)(2,1)}, u32[]{:S(2)}) copy-start(bf16[1,1024,256]{2,1,0:T(8,128)(2,1)} %param.5) | copy-start | bytes 1572868
  3.3 0.7 %copy-start.2 = (bf16[1,2,1024]{2,1,0:T(2,128)(2,1)S(1)}, bf16[1,2,1024]{2,1,0:T(2,128)(2,1)}, u32[]{:S(2)}) copy-start(bf16[1,2,1024]{2,1,0:T(2,128)(2,1)} %param.6) | copy-start | bytes 12292
  4.0 0.7 %copy-start.3 = (bf16[8,256]{1,0:T(8,128)(2,1)S(1)}, bf16[8,256]{1,0:T(8,128)(2,1)}, u32[]{:S(2)}) copy-start(bf16[8,256]{1,0:T(8,128)(2,1)} %phi_h.1) | copy-start | bytes 12292

commit v2 on v0

v2 whole, which is shorter than its diff:
```python
import contextlib
import functools

import jax
import jax.numpy as jnp
from jax import lax
from jax.experimental import pallas as pl
from jax.experimental.pallas import tpu as pltpu
from jax.sharding import Mesh
from jax.sharding import PartitionSpec as P

SEQ = ("seq_0", "seq_1", "seq_2")
MESH = pl.DeviceIdType.MESH
F32 = jnp.float32
BF16 = jnp.bfloat16
NT = (((1,), (1,)), ((), ()))


def far_first(n):
    return sorted(range(1, n), key=lambda k: (-min(k, n - k), k))


def kernel(
    n, nx, tok_h, log_h, g_h, phi_h, tg_o, pg_o,
    tok, tokT, logv, p, wg, dr, u, w, phim,
    g_other, p_other, l1, gh, ph, st_a, st_m, st_b,
    asnd, arcv, bsnd, brcv, bsum, r, rrcv, xs, xbuf, tgs, tgr,
    lsem, ssem, rsem, osem,
):
    open_scope = contextlib.ExitStack()

    def phase(name):
        open_scope.close()
        open_scope.enter_context(jax.named_scope(name))

    phase("greet")
    z, y, c, x = (lax.axis_index(a) for a in (*SEQ, "batch"))
    other = 1 - c
    a = z * other + y * c
    b = y * other + z * c
    _, ts, d = tok.shape
    sl = logv.shape[2]
    half = d // 2
    rows = d // (n * n)
    tile = min(256, ts)
    order = far_first(n)

    def along_a(k, core):
        return (lax.rem(z + k * other, n), lax.rem(y + k * c, n), core, x)

    def along_b(k, core):
        return (lax.rem(z + k * c, n), lax.rem(y + k * other, n), core, x)

    def along_x(k, core):
        return (z, y, core, lax.rem(x + k, nx))

    partner = (z, y, other, x)

    def send(src, dst, s, q, to):
        pltpu.make_async_remote_copy(
            src_ref=src, dst_ref=dst, send_sem=s, recv_sem=q, device_id=to, device_id_type=MESH
        ).start()

    def await_bytes(ref, sem):
        pltpu.make_async_copy(ref, ref, sem).wait()

    mine = pl.ds(pl.multiple_of(c * half, half), half)
    theirs = pl.ds(pl.multiple_of(other * half, half), half)
    my_slots = pl.ds(pl.multiple_of(c * sl, sl), sl)
    their_slots = pl.ds(pl.multiple_of(other * sl, sl), sl)
    loads = [
        pltpu.make_async_copy(g_h.at[:, mine], l1.at[b, c], lsem.at[0]),
        pltpu.make_async_copy(g_h.at[:, theirs], g_other, lsem.at[1]),
        pltpu.make_async_copy(phi_h.at[:, my_slots], ph.at[a, b, c], lsem.at[2]),
        pltpu.make_async_copy(phi_h.at[:, their_slots], p_other, lsem.at[3]),
        pltpu.make_async_copy(log_h.at[:, my_slots], logv.at[0], lsem.at[4]),
        pltpu.make_async_copy(tok_h, tok.at[0], lsem.at[5]),
    ]
    for one in loads:
        one.start()

    barrier = pltpu.get_barrier_semaphore()
    peers = [partner]
    for core in (c, other):
        for k in range(1, n):
            peers += [along_a(k, core), along_b(k, core)]
        peers += [along_x(k, core) for k in range(1, nx)]
    for to in peers:
        pl.semaphore_signal(barrier, inc=1, device_id=to, device_id_type=MESH)
    loads[0].wait()
    loads[1].wait()
    pl.semaphore_wait(barrier, len(peers))

    phase("g1_send")
    for k in order:
        send(l1.at[b, c], l1.at[b, c], ssem.at[0], rsem.at[0], along_b(k, c))
        send(g_other, l1.at[a, c], ssem.at[1], rsem.at[1], along_a(k, other))
    send(g_other, l1.at[a, c], ssem.at[1], rsem.at[1], partner)
    send(log_h.at[:, their_slots], logv.at[1], ssem.at[2], rsem.at[2], partner)
    loads[2].wait()
    loads[3].wait()
    for k in order:
        send(ph.at[a, b, c], ph.at[a, b, c], ssem.at[3], rsem.at[3], along_b(k, c))
        send(p_other, ph.at[b, a, c], ssem.at[4], rsem.at[4], along_a(k, other))
    send(p_other, ph.at[b, a, c], ssem.at[4], rsem.at[4], partner)
    send(tok_h, tok.at[1], ssem.at[5], rsem.at[5], partner)

    phase("peak")
    loads[4].wait()
    await_bytes(logv.at[1], rsem.at[2])
    peak = jnp.max(logv[...].astype(F32), axis=(0, 1))[None]
    total = jnp.zeros((1, sl), F32)
    for i in range(2):
        raw = jnp.exp(logv[i].astype(F32) - peak)
        p[i] = raw
        total = total + jnp.sum(raw, axis=0, keepdims=True)
    blank = jnp.zeros((2, sl), F32)
    st_a[a] = jnp.concatenate([peak, total, blank], axis=0)
    for k in order:
        send(st_a.at[a], st_a.at[a], ssem.at[6], rsem.at[6], along_a(k, c))

    lanes = n * rows

    def turn(i):
        for j in range(n):
            blk = tok[i, :, j * lanes : (j + 1) * lanes].T
            for m in range(n):
                ja = j * other + m * c
                jb = m * other + j * c
                row = (lax.rem(ja - a + 2 * n - 1, n) * n + jb) * rows
                tokT[pl.ds(pl.multiple_of(row, rows), rows), i * ts : (i + 1) * ts] = blk[
                    m * rows : (m + 1) * rows
                ]

    phase("turn0")
    loads[5].wait()
    turn(0)

    phase("g1_wait")
    await_bytes(l1.at[pl.ds(0, n - 1), 0], rsem.at[0])
    await_bytes(l1.at[:, 0], rsem.at[1])
    nh = n // 2
    near = lax.div(z, nh)
    zz = lax.rem(z, nh)

    @pl.when(c == 0)
    def _():
        for k in order:
            send(l1, gh.at[0, zz], ssem.at[7], rsem.at[7], along_a(k, near))

        @pl.when(near == 0)
        def _():
            pltpu.make_async_copy(l1, gh.at[0, zz], rsem.at[7]).start()

        @pl.when(near == 1)
        def _():
            send(l1, gh.at[0, zz], ssem.at[8], rsem.at[7], partner)

    @pl.when(c == 1)
    def _():
        for k in order:
            for q in range(2):
                send(
                    l1.at[pl.ds(q * nh, nh)], gh.at[1, :, y], ssem.at[7], rsem.at[8],
                    along_a(k, q),
                )
        send(l1.at[pl.ds(0, nh)], gh.at[1, :, y], ssem.at[8], rsem.at[8], partner)
        pltpu.make_async_copy(l1.at[pl.ds(nh, nh)], gh.at[1, :, y], rsem.at[8]).start()

    phase("phi_send")
    await_bytes(ph.at[0, pl.ds(0, n - 1), 0], rsem.at[3])
    await_bytes(ph.at[0, :, 0], rsem.at[4])
    for k in order:
        send(ph.at[a], ph.at[a], ssem.at[9], rsem.at[9], along_a(k, c))

    phase("turn1")
    await_bytes(tok.at[1], rsem.at[5])
    turn(1)

    phase("ml_wait")
    await_bytes(st_a.at[pl.ds(0, n - 1)], rsem.at[6])
    tops = [st_a[i, 0:1] for i in range(n)]
    ring_peak = functools.reduce(jnp.maximum, tops)
    ring_total = sum(st_a[i, 1:2] * jnp.exp(t - ring_peak) for i, t in enumerate(tops))
    to_ring = jnp.exp(peak - ring_peak)

    def weigh_ring(i):
        dr[i * ts : (i + 1) * ts] = (p[i] * to_ring).astype(BF16)

    weigh_ring(0)
    weigh_ring(1)

    blk = n * rows

    def reduce_first(snd, rcv, s, q):
        starts = sorted(range(0, n, 2), key=lambda i: -max(min(i + 1, n - i - 1), min(i + 2, n - i - 2)))
        for start in starts:
            res = jnp.dot(
                tokT[start * blk : (start + 2) * blk], dr[...], preferred_element_type=F32
            )
            for i in sorted(range(start, start + 2), key=lambda i: -min(i + 1, n - i - 1)):
                part = res[(i - start) * blk : (i - start + 1) * blk]
                if i == n - 1:
                    own = part
                else:
                    snd[i] = part.astype(BF16)
                    send(snd.at[i], rcv.at[i], s, q, along_a(i + 1, c))
        return own

    phase("b_send")
    bsum[...] = reduce_first(bsnd, brcv, ssem.at[10], rsem.at[10])

    phase("g2_wait")
    await_bytes(gh.at[0], rsem.at[7])
    await_bytes(gh.at[1], rsem.at[8])
    phase("weigh")
    per = n * 2 * gh.shape[4]
    for h in range(2):
        for i in range(nh):
            parts = [gh[h, i, j, k].astype(F32) for j in range(n) for k in range(2)]
            w[i * per : (i + 1) * per, h * half : (h + 1) * half] = jnp.concatenate(
                parts, axis=0
            ).astype(BF16)

    dots = jnp.zeros((1, sl), F32)
    for i in range(2):

        def weigh(j, acc, i=i):
            at = pl.ds(pl.multiple_of(j * tile, tile), tile)
            v = lax.dot_general(tok[i, at, :], w[0:sl, :], NT, preferred_element_type=F32)
            wg[i, at, :] = v
            return acc + jnp.sum(p[i, at, :] * v, axis=0, keepdims=True)

        dots = lax.fori_loop(0, ts // tile, weigh, dots)

    phase("mean")
    st_m[a] = jnp.concatenate([dots * to_ring, jnp.zeros((3, sl), F32)], axis=0)
    for k in order:
        send(st_m.at[a], st_m.at[a], ssem.at[11], rsem.at[11], along_a(k, c))
    await_bytes(st_m.at[pl.ds(0, n - 1)], rsem.at[11])
    ring_dots = sum(st_m[i, 0:1] for i in range(n))
    center0 = ring_dots / ring_total
    st_b[b] = jnp.concatenate([ring_peak, ring_total, ring_dots, blank[:1]], axis=0)
    for k in order:
        send(st_b.at[b], st_b.at[b], ssem.at[12], rsem.at[12], along_b(k, c))
    phase("a_send")
    for i in range(2):

        def grade(j, carry, i=i):
            at = pl.ds(pl.multiple_of(j * tile, tile), tile)
            to = pl.ds(pl.multiple_of(i * ts + j * tile, tile), tile)
            dr[to, :] = (p[i, at, :] * to_ring * (wg[i, at, :] - center0)).astype(BF16)
            return carry

        lax.fori_loop(0, ts // tile, grade, 0)
    own = reduce_first(asnd, arcv, ssem.at[13], rsem.at[13])

    phase("b_sum")
    await_bytes(brcv, rsem.at[10])
    low = bsum[...]
    for i in range(n - 1):
        low = low + brcv[i].astype(F32)

    phase("stat_b")
    await_bytes(st_b.at[pl.ds(0, n - 1)], rsem.at[12])
    tops = [st_b[i, 0:1] for i in range(n)]
    top = functools.reduce(jnp.maximum, tops)
    scales = [jnp.exp(t - top) for t in tops]
    norm = sum(st_b[i, 1:2] * s for i, s in enumerate(scales))
    center = sum(st_b[i, 2:3] * s for i, s in enumerate(scales)) / norm
    ring_scale = jnp.exp(ring_peak - top) / norm
    dev_scale = jnp.exp(peak - top) / norm
    for i in range(2):

        def settle(j, carry, i=i):
            at = pl.ds(pl.multiple_of(j * tile, tile), tile)
            dispatch = p[i, at, :] * dev_scale
            u[i, at, 0:sl] = dispatch.astype(BF16)
            u[i, at, sl : 2 * sl] = (dispatch * (wg[i, at, :] - center)).astype(BF16)
            return carry

        lax.fori_loop(0, ts // tile, settle, 0)
    low = low * (center - center0)

    phase("a_wait")
    await_bytes(arcv, rsem.at[13])
    for i in range(n - 1):
        own = own + arcv[i].astype(F32)
    r[...] = ((own - low) * ring_scale).reshape(n, rows, sl)
    for k in order:
        send(r.at[lax.rem(b + k, n)], rrcv.at[k - 1], ssem.at[14], rsem.at[14], along_b(k, c))

    phase("phi_wait")
    await_bytes(ph.at[pl.ds(0, n - 1)], rsem.at[9])
    for i in range(n):
        for j in range(n):
            at = ph.at[i * other + j * c, j * other + i * c]
            phim[(i * n + j) * rows : (i * n + j + 1) * rows] = at[...].astype(F32).reshape(rows, sl)
    w[sl : 2 * sl, :] = phim[...].T.astype(BF16)
    phase("emit_other")
    grad_scale = float(ts * n * n * 2 // 16)

    def emit_other(j, carry):
        at = pl.ds(pl.multiple_of(j * tile, tile), tile)
        s = jnp.dot(u[1, at, :], w[...], preferred_element_type=F32)
        tgs[at, :] = s.astype(BF16)
        send(tgs.at[at], tgr.at[at], osem.at[0], osem.at[1 + j], partner)
        return carry

    lax.fori_loop(0, ts // tile, emit_other, 0)

    phase("r_wait")
    res = r[b]
    await_bytes(rrcv, rsem.at[14])
    for k in range(n - 1):
        res = res + rrcv[k]
    xs[...] = res.reshape(2, rows // 2, sl)
    spot = x * 2 + c
    for k in far_first(nx):
        send(xs.at[c], xbuf.at[spot], ssem.at[15], rsem.at[15], along_x(k, c))
        send(xs.at[other], xbuf.at[spot], ssem.at[16], rsem.at[15], along_x(k, other))
    send(xs.at[other], xbuf.at[spot], ssem.at[16], rsem.at[15], partner)
    xbuf[spot] = xs[c]

    phase("emit_own")

    def emit_own(j, carry):
        at = pl.ds(pl.multiple_of(j * tile, tile), tile)
        s = jnp.dot(u[0, at, :], w[...], preferred_element_type=F32)
        await_bytes(tgr.at[at], osem.at[1 + j])
        tgs_own = (grad_scale * (s + tgr[at, :].astype(F32))).astype(BF16)
        tok[0, at, :] = tgs_own
        pltpu.make_async_copy(tok.at[0, at], tg_o.at[at], lsem.at[0]).start()
        return carry

    lax.fori_loop(0, ts // tile, emit_own, 0)

    phase("x_wait")
    await_bytes(xbuf.at[pl.ds(0, 2 * nx - 1)], rsem.at[15])
    for h in range(2):
        res = xbuf[h]
        for i in range(1, nx):
            res = res + xbuf[2 * i + h]
        pg_o[:, h * sl : (h + 1) * sl] = res

    phase("drain")
    await_bytes(l1.at[pl.ds(0, n - 1), 0], ssem.at[0])
    await_bytes(l1.at[:, 0], ssem.at[1])
    await_bytes(logv.at[1], ssem.at[2])
    await_bytes(ph.at[0, pl.ds(0, n - 1), 0], ssem.at[3])
    await_bytes(ph.at[0, :, 0], ssem.at[4])
    await_bytes(tok.at[1], ssem.at[5])
    await_bytes(st_a.at[pl.ds(0, n - 1)], ssem.at[6])
    await_bytes(gh.at[:, :, pl.ds(0, n - 1)], ssem.at[7])

    @pl.when((c == 0) & (near == 1))
    def _():
        await_bytes(l1, ssem.at[8])

    @pl.when(c == 1)
    def _():
        await_bytes(l1.at[pl.ds(0, nh)], ssem.at[8])

    await_bytes(ph.at[pl.ds(0, n - 1)], ssem.at[9])
    await_bytes(brcv, ssem.at[10])
    await_bytes(st_m.at[pl.ds(0, n - 1)], ssem.at[11])
    await_bytes(st_b.at[pl.ds(0, n - 1)], ssem.at[12])
    await_bytes(arcv, ssem.at[13])
    await_bytes(rrcv, ssem.at[14])
    await_bytes(xbuf.at[pl.ds(0, nx - 1)], ssem.at[15])
    await_bytes(xbuf.at[pl.ds(0, nx)], ssem.at[16])
    await_bytes(tgs, osem.at[0])
    await_bytes(tok.at[0], lsem.at[0])
    open_scope.close()


def per_device(n, nx, tokens, logits, slot_grad, phi_param):
    tokens, logits, slot_grad = tokens[0], logits[0], slot_grad[0]
    ts, d = tokens.shape
    sl = logits.shape[1] // 2
    rows = d // (n * n)
    gs = slot_grad.shape[0]
    half = d // 2
    tile = min(256, ts)
    vm, dma = pltpu.VMEM, pltpu.SemaphoreType.DMA
    any_spec = pl.BlockSpec(memory_space=pl.ANY)
    scratch = [
        vm((2, ts, d), BF16), vm((d, 2 * ts), BF16), vm((2, ts, sl), BF16),
        vm((2, ts, sl), F32), vm((2, ts, sl), F32), vm((2 * ts, sl), BF16),
        vm((2, ts, 2 * sl), BF16), vm((2 * sl, d), BF16), vm((d, sl), F32),
        vm((gs, half), BF16), vm((rows // 2, sl), BF16),
        vm((n, 2, gs, half), BF16), vm((2, n // 2, n, 2, gs, half), BF16),
        vm((n, n, 2, rows // 2, sl), BF16),
        vm((n, 4, sl), F32), vm((n, 4, sl), F32), vm((n, 4, sl), F32),
        vm((n - 1, n * rows, sl), BF16), vm((n - 1, n * rows, sl), BF16),
        vm((n - 1, n * rows, sl), BF16), vm((n - 1, n * rows, sl), BF16),
        vm((n * rows, sl), F32), vm((n, rows, sl), F32), vm((n - 1, rows, sl), F32),
        vm((2, rows // 2, sl), F32), vm((2 * nx, rows // 2, sl), F32),
        vm((ts, d), BF16), vm((ts, d), BF16),
        dma((6,)), dma((17,)), dma((16,)), dma((1 + ts // tile,)),
    ]
    token_grad, phi_grad = pl.pallas_call(
        functools.partial(kernel, n, nx),
        out_shape=(
            jax.ShapeDtypeStruct((ts, d), BF16),
            jax.ShapeDtypeStruct((rows // 2, 2 * sl), F32),
        ),
        in_specs=[any_spec] * 4,
        out_specs=(any_spec, pl.BlockSpec(memory_space=pltpu.VMEM)),
        scratch_shapes=scratch,
        compiler_params=pltpu.CompilerParams(
            collective_id=0, has_side_effects=True, vmem_limit_bytes=67043328
        ),
        name="moe_dispatch_backward",
    )(tokens, logits, slot_grad, phi_param)
    return token_grad[None], phi_grad


def solution(mesh):
    count, nx = mesh.devices.shape
    n = 8 if count == 128 else 2
    finer = Mesh(mesh.devices.reshape(n, n, 2, nx), (*SEQ, "batch"))
    in_specs = (P("batch", SEQ, None), P("batch", SEQ, None), P("batch", SEQ, None), P(SEQ, None))
    out_specs = (P("batch", SEQ, None), P(SEQ, None))
    return jax.shard_map(
        functools.partial(per_device, n, nx),
        mesh=finer, in_specs=in_specs, out_specs=out_specs, check_vma=False,
    )
```

time: 259 us -> 53 us (0.20)
  the two profiles are of different devices: /device:TPU:2 before, /device:TPU:1 now
where the time goes in v2:
time: 53 us; the launch traced here: 52.9 us
  Pallas kernels  48.5 us (92%)
  local copies, waits for them, and re-layouts  3.69 us (7%)
  between operations  0.65 us (1%)
    pallas_call x1, Pallas kernels, per_device(): pl.pallas_call(functools.partial(kernel, n, nx), out_shape=(jax.ShapeDtyp...  48.5 us
    unnamed x4, local copies, waits for them, and re-layouts  3.69 us

profile of v2, /device:TPU:1, one launch (start us, length us, event | category | flops | bytes accessed | tf_op | source)
XLA Modules:
  0.0 52.9 jit_solution(18053118621346587683)
XLA Ops:
  0.6 48.5 %moe_dispatch_backward.1 = (bf16[1024,1024]{1,0:T(8,128)(2,1)}, f32[8,256]{1,0:T(8,128)}) custom-call(bf16[1024,1024]{1,0:T(8,128)(2,1)} %bitcast.4, bf16[1024,256]{1,0:T(8,128)(2,1)} %bitcast.6, bf16[2,1024]{1,0:T(2,128)(2,1)} %bitcast.7, bf16[8,256]{1,0:T(8,128)(2,1)} %phi_h.1), custom_call_target="tpu_custom_call" | custom-call | tf_op jit(solution)/shard_map/moe_dispatch_backward/pallas_call | solution.py:402
  49.2 0.0 copy-start
  49.2 3.1 %copy.8 = bf16[1,1024,1024]{2,1,0:T(8,128)(2,1)} copy(bf16[1,1024,1024]{2,1,0:T(8,128)(2,1)} %bitcast.5) | data formatting | bytes 4194304
  52.3 0.0 copy-done
  52.3 0.6 %copy.9 = f32[8,256]{1,0:T(8,128)} copy(f32[8,256]{1,0:T(8,128)S(1)} %copy-done) | data formatting | bytes 16384
Async XLA Ops:
  49.2 3.1 %copy-start = (f32[8,256]{1,0:T(8,128)S(1)}, f32[8,256]{1,0:T(8,128)}, u32[]{:S(2)}) copy-start(f32[8,256]{1,0:T(8,128)} %get-tuple-element.9) | copy-start | bytes 24580

commit v3 on v2

v3 whole, which is shorter than its diff:
```python
import contextlib
import functools

import jax
import jax.numpy as jnp
from jax import lax
from jax.experimental import pallas as pl
from jax.experimental.pallas import tpu as pltpu
from jax.sharding import Mesh
from jax.sharding import PartitionSpec as P

SEQ = ("seq_0", "seq_1", "seq_2")
MESH = pl.DeviceIdType.MESH
F32 = jnp.float32
BF16 = jnp.bfloat16
NT = (((1,), (1,)), ((), ()))


def far_first(n):
    return sorted(range(1, n), key=lambda k: (-min(k, n - k), k))


def kernel(
    n, nx, tok_h, log_h, g_h, phi_h, tg_o, pg_o,
    tok, tokT, logv, p, wg, dr, u, w, phim,
    g_other, p_other, l1, gh, ph, st_a, st_m, st_b, fin_out, fin,
    asnd, arcv, bsnd, brcv, mine_b, bhl, r, rrcv, xs, xbuf, tgs, tgr,
    lsem, ssem, rsem, gsem, osem,
):
    open_scope = contextlib.ExitStack()

    def phase(name):
        open_scope.close()
        open_scope.enter_context(jax.named_scope(name))

    phase("greet")
    z, y, c, x = (lax.axis_index(a) for a in (*SEQ, "batch"))
    other = 1 - c
    a = z * other + y * c
    b = y * other + z * c
    _, ts, d = tok.shape
    sl = logv.shape[2]
    half = d // 2
    rows = d // (n * n)
    tile = min(256, ts)
    order = far_first(n)

    def along_a(k, core):
        return (lax.rem(z + k * other, n), lax.rem(y + k * c, n), core, x)

    def along_b(k, core):
        return (lax.rem(z + k * c, n), lax.rem(y + k * other, n), core, x)

    def along_x(k, core):
        return (z, y, core, lax.rem(x + k, nx))

    partner = (z, y, other, x)

    def send(src, dst, s, q, to):
        pltpu.make_async_remote_copy(
            src_ref=src, dst_ref=dst, send_sem=s, recv_sem=q, device_id=to, device_id_type=MESH
        ).start()

    def await_bytes(ref, sem):
        pltpu.make_async_copy(ref, ref, sem).wait()

    mine = pl.ds(pl.multiple_of(c * half, half), half)
    theirs = pl.ds(pl.multiple_of(other * half, half), half)
    my_slots = pl.ds(pl.multiple_of(c * sl, sl), sl)
    their_slots = pl.ds(pl.multiple_of(other * sl, sl), sl)
    loads = [
        pltpu.make_async_copy(g_h.at[:, mine], l1.at[b, c], lsem.at[0]),
        pltpu.make_async_copy(g_h.at[:, theirs], g_other, lsem.at[1]),
        pltpu.make_async_copy(phi_h.at[:, my_slots], ph.at[a, b, c], lsem.at[2]),
        pltpu.make_async_copy(phi_h.at[:, their_slots], p_other, lsem.at[3]),
        pltpu.make_async_copy(log_h.at[:, my_slots], logv.at[0], lsem.at[4]),
        pltpu.make_async_copy(tok_h, tok.at[0], lsem.at[5]),
    ]
    loads[0].start()
    loads[1].start()

    barrier = pltpu.get_barrier_semaphore()
    peers = [partner]
    for k in order:
        for core in (c, other):
            peers += [along_a(k, core), along_b(k, core)]
    for k in range(1, nx):
        peers += [along_x(k, core) for core in (c, other)]
    for to in peers:
        pl.semaphore_signal(barrier, inc=1, device_id=to, device_id_type=MESH)
    for one in loads[2:]:
        one.start()
    loads[0].wait()
    loads[1].wait()
    pl.semaphore_wait(barrier, len(peers))

    def along_z(k, core):
        return (lax.rem(z + k, n), y, core, x)

    def along_y(k, core):
        return (z, lax.rem(y + k, n), core, x)

    phase("g1_send")
    for k in order:
        send(l1.at[b, c], l1.at[b, c], ssem.at[0], rsem.at[0], along_b(k, c))
        send(g_other, l1.at[a, c], ssem.at[1], rsem.at[1], along_a(k, other))
    send(g_other, l1.at[a, c], ssem.at[1], rsem.at[1], partner)
    send(log_h.at[:, their_slots], logv.at[1], ssem.at[2], rsem.at[2], partner)
    loads[2].wait()
    loads[3].wait()
    for k in order:
        send(ph.at[a, b, c], ph.at[a, b, c], ssem.at[3], rsem.at[3], along_b(k, c))
        send(p_other, ph.at[b, a, c], ssem.at[4], rsem.at[4], along_a(k, other))
    send(p_other, ph.at[b, a, c], ssem.at[4], rsem.at[4], partner)
    send(tok_h, tok.at[1], ssem.at[5], rsem.at[5], partner)

    phase("peak")
    loads[4].wait()
    await_bytes(logv.at[1], rsem.at[2])
    peak = jnp.max(logv[...].astype(F32), axis=(0, 1))[None]
    total = jnp.zeros((1, sl), F32)
    for i in range(2):
        raw = jnp.exp(logv[i].astype(F32) - peak)
        p[i] = raw
        total = total + jnp.sum(raw, axis=0, keepdims=True)
    blank = jnp.zeros((2, sl), F32)
    st_a[a] = jnp.concatenate([peak, total, blank], axis=0)
    for k in order:
        send(st_a.at[a], st_a.at[a], ssem.at[6], rsem.at[6], along_a(k, c))

    lanes = n * rows

    def turn(i):
        for j in range(n):
            blk = tok[i, :, j * lanes : (j + 1) * lanes].T
            for m in range(n):
                ja = j * other + m * c
                jb = m * other + j * c
                row = (lax.rem(ja - a + 2 * n - 1, n) * n + jb) * rows
                tokT[pl.ds(pl.multiple_of(row, rows), rows), i * ts : (i + 1) * ts] = blk[
                    m * rows : (m + 1) * rows
                ]

    phase("turn0")
    loads[5].wait()
    turn(0)

    phase("g1_wait")
    await_bytes(l1.at[pl.ds(0, n - 1), 0], rsem.at[0])
    await_bytes(l1.at[:, 0], rsem.at[1])
    nh = n // 2
    near = lax.div(z, nh)
    zz = lax.rem(z, nh)

    @pl.when(c == 0)
    def _():
        for k in order:
            send(l1, gh.at[0, zz], ssem.at[7], gsem.at[zz], along_a(k, near))

        @pl.when(near == 0)
        def _():
            pltpu.make_async_copy(l1, gh.at[0, zz], gsem.at[zz]).start()

        @pl.when(near == 1)
        def _():
            send(l1, gh.at[0, zz], ssem.at[8], gsem.at[zz], partner)

    @pl.when(c == 1)
    def _():
        for k in order:
            for q in range(2):
                send(
                    l1.at[pl.ds(q * nh, nh)], gh.at[1, :, y], ssem.at[7], rsem.at[8],
                    along_a(k, q),
                )
        send(l1.at[pl.ds(0, nh)], gh.at[1, :, y], ssem.at[8], rsem.at[8], partner)
        pltpu.make_async_copy(l1.at[pl.ds(nh, nh)], gh.at[1, :, y], rsem.at[8]).start()

    phase("phi_send")
    await_bytes(ph.at[0, pl.ds(0, n - 1), 0], rsem.at[3])
    await_bytes(ph.at[0, :, 0], rsem.at[4])
    for k in order:
        send(ph.at[a], ph.at[a], ssem.at[9], rsem.at[9], along_a(k, c))

    phase("turn1")
    await_bytes(tok.at[1], rsem.at[5])
    turn(1)

    phase("ml_wait")
    await_bytes(st_a.at[pl.ds(0, n - 1)], rsem.at[6])
    tops = [st_a[i, 0:1] for i in range(n)]
    ring_peak = functools.reduce(jnp.maximum, tops)
    ring_total = sum(st_a[i, 1:2] * jnp.exp(t - ring_peak) for i, t in enumerate(tops))
    to_ring = jnp.exp(peak - ring_peak)

    mass = jnp.zeros((1, sl), F32)
    for i in range(2):
        low = (p[i] * to_ring).astype(BF16)
        dr[i * ts : (i + 1) * ts] = low
        mass = mass + jnp.sum(low.astype(F32), axis=0, keepdims=True)

    blk = n * rows

    def chip_sums(visit):
        for start in sorted(range(0, n, 2), key=lambda i: -max(min(i + 1, n - i - 1), min(i + 2, n - i - 2))):
            res = jnp.dot(
                tokT[start * blk : (start + 2) * blk], dr[...], preferred_element_type=F32
            )
            for i in sorted(range(start, start + 2), key=lambda i: -min(i + 1, n - i - 1)):
                visit(i, res[(i - start) * blk : (i - start + 1) * blk])

    def hand_on(i, snd, rcv, s, t, q):
        if i < n - 1:
            send(snd.at[i], rcv.at[c, i], ssem.at[s], rsem.at[q + c], along_a(i + 1, 1))
            return

        @pl.when(c == 0)
        def _():
            send(snd.at[i], rcv.at[0, i], ssem.at[t], rsem.at[q], partner)

        @pl.when(c == 1)
        def _():
            pltpu.make_async_copy(snd.at[i], rcv.at[1, i], rsem.at[q + 1]).start()

    def b_visit(i, part):
        high = part.astype(BF16)
        bsnd[i] = high
        hand_on(i, bsnd, brcv, 10, 22, 10)
        rest = (part - high.astype(F32)).astype(BF16)
        ja = lax.rem(a + i + 1, n)
        for jb in range(n):
            row = ((ja * other + jb * c) * n + jb * other + ja * c) * rows
            at = pl.ds(pl.multiple_of(row, rows), rows)
            bhl[at, 0:sl] = high[jb * rows : (jb + 1) * rows]
            bhl[at, sl : 2 * sl] = rest[jb * rows : (jb + 1) * rows]

    def a_visit(i, part):
        asnd[i] = part.astype(BF16)
        hand_on(i, asnd, arcv, 13, 14, 12)

    phase("b_send")
    chip_sums(b_visit)

    per = n * 2 * gh.shape[4]

    def gather_rows(h, i):
        parts = [gh[h, i, j, k].astype(F32) for j in range(n) for k in range(2)]
        w[i * per : (i + 1) * per, h * half : (h + 1) * half] = jnp.concatenate(
            parts, axis=0
        ).astype(BF16)

    phase("g2_wait")
    for i in range(nh):
        await_bytes(gh.at[0, i], gsem.at[i])
        gather_rows(0, i)
    await_bytes(gh.at[1], rsem.at[8])
    phase("dots")
    for i in range(nh):
        gather_rows(1, i)
    prod = jnp.dot(w[0:sl, :], bhl[...], preferred_element_type=F32)
    at_row = lax.broadcasted_iota(jnp.int32, (sl, 2 * sl), 0)
    at_col = lax.broadcasted_iota(jnp.int32, (sl, 2 * sl), 1)
    prod = jnp.where((at_row == at_col) | (at_row + sl == at_col), prod, 0.0)
    prod = jnp.sum(prod, axis=0, keepdims=True)
    dots = prod[:, 0:sl] + prod[:, sl : 2 * sl]
    st_m[c, a] = jnp.concatenate([dots, mass, ring_peak, ring_total], axis=0)
    for k in order:
        send(st_m.at[c, a], st_m.at[c, a], ssem.at[11], rsem.at[14 + c], along_a(k, 1))

    @pl.when(c == 0)
    def _():
        send(st_m.at[c, a], st_m.at[c, a], ssem.at[12], rsem.at[14], partner)

    def mean_of(total, weight):
        some = weight > 0.0
        return jnp.where(some, total / jnp.where(some, weight, 1.0), 0.0)

    center_dev = mean_of(dots, mass)

    phase("weigh")
    for i in range(2):
        for j in range(ts // tile):
            at = pl.ds(j * tile, tile)
            v = lax.dot_general(tok[i, at, :], w[0:sl, :], NT, preferred_element_type=F32)
            wg[i, at, :] = v
            dr[pl.ds(i * ts + j * tile, tile), :] = (
                p[i, at, :] * to_ring * (v - center_dev)
            ).astype(BF16)
    phase("a_send")
    chip_sums(a_visit)

    phase("b_wait")
    at_b = (y, z)
    to_b = (along_y, along_z)

    def spread(h, q, value):
        r[q, h] = value.reshape(n, rows, sl)
        for k in order:
            send(
                r.at[q, h, lax.rem(at_b[h] + k, n)], rrcv.at[q, h, at_b[h]], ssem.at[21],
                rsem.at[17 + q], to_b[h](k, 1),
            )
        rrcv[q, h, at_b[h]] = r[q, h, at_b[h]]

    @pl.when(c == 1)
    def _():
        await_bytes(brcv.at[0], rsem.at[10])
        await_bytes(brcv.at[1], rsem.at[11])
        for h in range(2):
            spread(h, 0, sum(brcv[h, i].astype(F32) for i in range(n)))
        phase("m_wait")
        await_bytes(st_m.at[0], rsem.at[14])
        await_bytes(st_m.at[1, pl.ds(0, n - 1)], rsem.at[15])
        ring_at = (z, y)
        for h in range(2):
            sums = [sum(st_m[h, i, q : q + 1] for i in range(n)) for q in range(2)]
            st_b[h, at_b[h]] = jnp.concatenate([*sums, st_m[h, 0, 2:4]], axis=0)
            for k in order:
                spot = st_b.at[h, at_b[h]]
                send(spot, spot, ssem.at[19], rsem.at[16], to_b[h](k, 1))
        for h in range(2):
            low = jnp.zeros((blk, sl), F32)
            for i in range(n):
                peer = lax.rem(ring_at[h] + 2 * n - 1 - i, n)
                low = low + mean_of(st_m[h, peer, 0:1], st_m[h, peer, 1:2]) * brcv[h, i].astype(F32)
            mine_b[h] = low
        phase("a_wait")
        await_bytes(arcv.at[0], rsem.at[12])
        await_bytes(arcv.at[1], rsem.at[13])
        for h in range(2):
            res = mine_b[h]
            for i in range(n):
                res = res + arcv[h, i].astype(F32)
            spread(h, 1, res)
        phase("centers")
        await_bytes(st_b.at[:, pl.ds(0, n - 1)], rsem.at[16])
        for h in range(2):
            tops = [st_b[h, i, 2:3] for i in range(n)]
            top = functools.reduce(jnp.maximum, tops)
            scales = [jnp.exp(t - top) for t in tops]
            dot_sum, weight, norm = (
                sum(st_b[h, i, q : q + 1] * s for i, s in enumerate(scales)) for q in (0, 1, 3)
            )
            fin_out[h] = jnp.concatenate([dot_sum / weight, top, norm, blank[:1]], axis=0)
        send(fin_out.at[0], fin, ssem.at[20], rsem.at[19], partner)
        fin[...] = fin_out[1]

    @pl.when(c == 0)
    def _():
        await_bytes(fin, rsem.at[19])

    phase("settle")
    center = fin[0:1]
    dev_scale = jnp.exp(peak - fin[1:2]) / fin[2:3]
    for i in range(2):

        def settle(j, carry, i=i):
            at = pl.ds(pl.multiple_of(j * tile, tile), tile)
            dispatch = p[i, at, :] * dev_scale
            u[i, at, 0:sl] = dispatch.astype(BF16)
            u[i, at, sl : 2 * sl] = (dispatch * (wg[i, at, :] - center)).astype(BF16)
            return carry

        lax.fori_loop(0, ts // tile, settle, 0)

    phase("phi_wait")
    await_bytes(ph.at[pl.ds(0, n - 1)], rsem.at[9])
    for i in range(n):
        for j in range(n):
            at = ph.at[i * other + j * c, j * other + i * c]
            phim[(i * n + j) * rows : (i * n + j + 1) * rows] = at[...].astype(F32).reshape(rows, sl)
    w[sl : 2 * sl, :] = phim[...].T.astype(BF16)
    phase("emit_other")
    grad_scale = float(ts * n * n * 2 // 16)

    def emit_other(j, carry):
        at = pl.ds(pl.multiple_of(j * tile, tile), tile)
        s = jnp.dot(u[1, at, :], w[...], preferred_element_type=F32)
        tgs[at, :] = s.astype(BF16)
        send(tgs.at[at], tgr.at[at], osem.at[0], osem.at[1 + j], partner)
        return carry

    lax.fori_loop(0, ts // tile, emit_other, 0)

    phase("r_wait")

    @pl.when(c == 1)
    def _():
        await_bytes(rrcv.at[0, :, pl.ds(0, n - 1)], rsem.at[17])
        await_bytes(rrcv.at[1, :, pl.ds(0, n - 1)], rsem.at[18])
        for h in range(2):
            res = jnp.zeros((rows, sl), F32)
            for i in range(n):
                ring_scale = jnp.exp(st_b[h, i, 2:3] - fin_out[h, 1:2]) / fin_out[h, 2:3]
                res = res + (rrcv[1, h, i] - fin_out[h, 0:1] * rrcv[0, h, i]) * ring_scale
            xs[:, :, h * sl : (h + 1) * sl] = res.reshape(2, rows // 2, sl)
        for k in far_first(nx):
            for core in range(2):
                send(xs.at[core], xbuf.at[x], ssem.at[15], rsem.at[20], along_x(k, core))
        send(xs.at[0], xbuf.at[x], ssem.at[16], rsem.at[20], partner)
        xbuf[x] = xs[1]

    phase("emit_own")

    def emit_own(j, carry):
        at = pl.ds(pl.multiple_of(j * tile, tile), tile)
        s = jnp.dot(u[0, at, :], w[...], preferred_element_type=F32)
        await_bytes(tgr.at[at], osem.at[1 + j])
        tg_o[at, :] = (grad_scale * (s + tgr[at, :].astype(F32))).astype(BF16)
        return carry

    lax.fori_loop(0, ts // tile, emit_own, 0)

    phase("x_wait")
    @pl.when(c == 0)
    def _():
        await_bytes(xbuf, rsem.at[20])

    @pl.when(c == 1)
    def _():
        await_bytes(xbuf.at[pl.ds(0, nx - 1)], rsem.at[20])

    res = xbuf[0]
    for i in range(1, nx):
        res = res + xbuf[i]
    pg_o[...] = res

    phase("drain")
    await_bytes(l1.at[pl.ds(0, n - 1), 0], ssem.at[0])
    await_bytes(l1.at[:, 0], ssem.at[1])
    await_bytes(gh.at[:, :, pl.ds(0, n - 1)], ssem.at[7])
    await_bytes(logv.at[1], ssem.at[2])
    await_bytes(ph.at[0, pl.ds(0, n - 1), 0], ssem.at[3])
    await_bytes(ph.at[0, :, 0], ssem.at[4])
    await_bytes(tok.at[1], ssem.at[5])
    await_bytes(st_a.at[pl.ds(0, n - 1)], ssem.at[6])
    await_bytes(ph.at[pl.ds(0, n - 1)], ssem.at[9])
    await_bytes(brcv.at[0, pl.ds(0, n - 1)], ssem.at[10])
    await_bytes(st_m.at[0, pl.ds(0, n - 1)], ssem.at[11])
    await_bytes(arcv.at[0, pl.ds(0, n - 1)], ssem.at[13])
    await_bytes(tgs, osem.at[0])

    @pl.when((c == 0) & (near == 1))
    def _():
        await_bytes(l1, ssem.at[8])

    @pl.when(c == 0)
    def _():
        await_bytes(brcv.at[0, 0], ssem.at[22])
        await_bytes(arcv.at[0, 0], ssem.at[14])
        await_bytes(st_m.at[0, 0], ssem.at[12])

    @pl.when(c == 1)
    def _():
        await_bytes(l1.at[pl.ds(0, nh)], ssem.at[8])
        await_bytes(st_b.at[:, pl.ds(0, n - 1)], ssem.at[19])
        await_bytes(fin, ssem.at[20])
        await_bytes(rrcv.at[:, :, pl.ds(0, n - 1)], ssem.at[21])
        await_bytes(xbuf.at[pl.ds(0, nx - 1)], ssem.at[15])
        await_bytes(xbuf.at[pl.ds(0, nx - 1)], ssem.at[15])
        await_bytes(xbuf.at[0], ssem.at[16])

    open_scope.close()


def write_out(tg_v, pg_v, tg_o, pg_o, sem):
    parts = 8
    copies = [pltpu.make_async_copy(pg_v, pg_o, sem.at[parts])]
    size = tg_v.shape[0] // parts
    for i in range(parts):
        at = pl.ds(i * size, size)
        copies.append(pltpu.make_async_copy(tg_v.at[at], tg_o.at[at], sem.at[i]))
    for one in copies:
        one.start()
    for one in copies:
        one.wait()


def per_device(n, nx, tokens, logits, slot_grad, phi_param):
    tokens, logits, slot_grad = tokens[0], logits[0], slot_grad[0]
    ts, d = tokens.shape
    sl = logits.shape[1] // 2
    rows = d // (n * n)
    gs = slot_grad.shape[0]
    half = d // 2
    tile = min(256, ts)
    vm, dma = pltpu.VMEM, pltpu.SemaphoreType.DMA
    any_spec = pl.BlockSpec(memory_space=pl.ANY)
    scratch = [
        vm((2, ts, d), BF16), vm((d, 2 * ts), BF16), vm((2, ts, sl), BF16),
        vm((2, ts, sl), F32), vm((2, ts, sl), F32), vm((2 * ts, sl), BF16),
        vm((2, ts, 2 * sl), BF16), vm((2 * sl, d), BF16), vm((d, sl), F32),
        vm((gs, half), BF16), vm((rows // 2, sl), BF16),
        vm((n, 2, gs, half), BF16), vm((2, n // 2, n, 2, gs, half), BF16),
        vm((n, n, 2, rows // 2, sl), BF16),
        vm((n, 4, sl), F32), vm((2, n, 4, sl), F32), vm((2, n, 4, sl), F32),
        vm((2, 4, sl), F32), vm((4, sl), F32),
        vm((n, n * rows, sl), BF16), vm((2, n, n * rows, sl), BF16),
        vm((n, n * rows, sl), BF16), vm((2, n, n * rows, sl), BF16),
        vm((2, n * rows, sl), F32), vm((d, 2 * sl), BF16),
        vm((2, 2, n, rows, sl), F32), vm((2, 2, n, rows, sl), F32),
        vm((2, rows // 2, 2 * sl), F32), vm((nx, rows // 2, 2 * sl), F32),
        vm((ts, d), BF16), vm((ts, d), BF16),
        dma((6,)), dma((23,)), dma((21,)), dma((n // 2,)), dma((1 + ts // tile,)),
    ]
    vm_spec = pl.BlockSpec(memory_space=pltpu.VMEM)
    token_grad, phi_grad = pl.pallas_call(
        functools.partial(kernel, n, nx),
        out_shape=(pltpu.VMEM((ts, d), BF16), pltpu.VMEM((rows // 2, 2 * sl), F32)),
        in_specs=[any_spec] * 4,
        out_specs=(vm_spec, vm_spec),
        scratch_shapes=scratch,
        compiler_params=pltpu.CompilerParams(
            collective_id=0, has_side_effects=True, vmem_limit_bytes=56000000
        ),
        name="moe_dispatch_backward",
    )(tokens, logits, slot_grad, phi_param)
    token_grad, phi_grad = pl.pallas_call(
        write_out,
        out_shape=(
            jax.ShapeDtypeStruct((ts, d), BF16),
            jax.ShapeDtypeStruct((rows // 2, 2 * sl), F32),
        ),
        in_specs=[any_spec, any_spec],
        out_specs=(any_spec, any_spec),
        scratch_shapes=[dma((9,))],
        compiler_params=pltpu.CompilerParams(vmem_limit_bytes=4 * 1024 * 1024),
        name="write_out",
    )(token_grad, phi_grad)
    return token_grad[None], phi_grad


def solution(mesh):
    count, nx = mesh.devices.shape
    n = round((count // 2) ** 0.5)
    finer = Mesh(mesh.devices.reshape(n, n, 2, nx), (*SEQ, "batch"))
    in_specs = (P("batch", SEQ, None), P("batch", SEQ, None), P("batch", SEQ, None), P(SEQ, None))
    out_specs = (P("batch", SEQ, None), P(SEQ, None))
    return jax.shard_map(
        functools.partial(per_device, n, nx),
        mesh=finer, in_specs=in_specs, out_specs=out_specs, check_vma=False,
    )
```

time: 53 us -> 45.5 us (0.86)
  Pallas kernels: 48.5 us -> 44.8 us
  local copies, waits for them, and re-layouts: 3.69 us -> 0 us
    pallas_call x1 -> x2, Pallas kernels: 48.5 us -> 44.8 us  [the longest x1 43.4 us: per_device(): pl.pallas_call(functools.partial(kernel, n, nx), out_shape=(pltpu.VMEM((t...]
    unnamed x4 -> x0, local copies, waits for them, and re-layouts: 3.69 us -> none
where the time goes in v3:
time: 45.5 us; the launch traced here: 45.4 us
  Pallas kernels  44.8 us (98%)
  between operations  0.64 us (1%)
    pallas_call x1, Pallas kernels, per_device(): pl.pallas_call(functools.partial(kernel, n, nx), out_shape=(pltpu.VMEM((t...  43.4 us
    pallas_call x1, Pallas kernels, per_device(): pl.pallas_call(write_out, out_shape=(jax.ShapeDtypeStruct((ts, d), BF16),...  1.39 us

profile of v3, /device:TPU:1, one launch (start us, length us, event | category | flops | bytes accessed | tf_op | source)
XLA Modules:
  0.0 45.4 jit_solution(11465024311450597060)
XLA Ops:
  0.6 43.4 %moe_dispatch_backward.1 = (bf16[1024,1024]{1,0:T(8,128)(2,1)S(1)}, f32[8,256]{1,0:T(8,128)S(1)}) custom-call(bf16[1024,1024]{1,0:T(8,128)(2,1)} %bitcast.4, bf16[1024,256]{1,0:T(8,128)(2,1)} %bitcast.5, bf16[2,1024]{1,0:T(2,128)(2,1)} %bitcast.6, bf16[8,256]{1,0:T(8,128)(2,1)} %phi_h.1), custom_call_target="tpu_custom_call" | custom-call | tf_op jit(solution)/shard_map/moe_dispatch_backward/pallas_call | solution.py:507
  44.0 1.4 %write_out.1 = (bf16[1024,1024]{1,0:T(8,128)(2,1)}, f32[8,256]{1,0:T(8,128)}) custom-call(bf16[1024,1024]{1,0:T(8,128)(2,1)S(1)} %get-tuple-element.6.tg_v, f32[8,256]{1,0:T(8,128)S(1)} %get-tuple-element.7.pg_v), custom_call_target="tpu_custom_call" | custom-call | tf_op jit(solution)/shard_map/write_out/pallas_call | solution.py:518

commit v4 on v3

--- a/solution.py
+++ b/solution.py
@@ -24,8 +24,8 @@
     n, nx, tok_h, log_h, g_h, phi_h, tg_o, pg_o,
     tok, tokT, logv, p, wg, dr, u, w, phim,
     g_other, p_other, l1, gh, ph, st_a, st_m, st_b, fin_out, fin,
-    asnd, arcv, bsnd, brcv, mine_b, bhl, r, rrcv, xs, xbuf, tgs, tgr,
-    lsem, ssem, rsem, gsem, osem,
+    asnd, arcv, bsnd, brcv, mine_b, bhl, r, rrcv, xs, xbuf, po, wo, pko,
+    lsem, ssem, rsem, gsem,
 ):
     open_scope = contextlib.ExitStack()
 
@@ -71,7 +71,7 @@
     loads = [
         pltpu.make_async_copy(g_h.at[:, mine], l1.at[b, c], lsem.at[0]),
         pltpu.make_async_copy(g_h.at[:, theirs], g_other, lsem.at[1]),
-        pltpu.make_async_copy(phi_h.at[:, my_slots], ph.at[a, b, c], lsem.at[2]),
+        pltpu.make_async_copy(phi_h.at[:, my_slots], ph.at[0, b, c], lsem.at[2]),
         pltpu.make_async_copy(phi_h.at[:, their_slots], p_other, lsem.at[3]),
         pltpu.make_async_copy(log_h.at[:, my_slots], logv.at[0], lsem.at[4]),
         pltpu.make_async_copy(tok_h, tok.at[0], lsem.at[5]),
@@ -109,9 +109,9 @@
     loads[2].wait()
     loads[3].wait()
     for k in order:
-        send(ph.at[a, b, c], ph.at[a, b, c], ssem.at[3], rsem.at[3], along_b(k, c))
-        send(p_other, ph.at[b, a, c], ssem.at[4], rsem.at[4], along_a(k, other))
-    send(p_other, ph.at[b, a, c], ssem.at[4], rsem.at[4], partner)
+        send(ph.at[0, b, c], ph.at[0, b, c], ssem.at[3], rsem.at[3], along_b(k, c))
+        send(p_other, ph.at[0, a, c], ssem.at[4], rsem.at[4], along_a(k, other))
+    send(p_other, ph.at[0, a, c], ssem.at[4], rsem.at[4], partner)
     send(tok_h, tok.at[1], ssem.at[5], rsem.at[5], partner)
 
     phase("peak")
@@ -179,8 +179,9 @@
     phase("phi_send")
     await_bytes(ph.at[0, pl.ds(0, n - 1), 0], rsem.at[3])
     await_bytes(ph.at[0, :, 0], rsem.at[4])
+    part = pl.ds(x * (n // nx), n // nx)
     for k in order:
-        send(ph.at[a], ph.at[a], ssem.at[9], rsem.at[9], along_a(k, c))
+        send(ph.at[0, part], ph.at[n - k, part], ssem.at[9], rsem.at[9], along_a(k, c))
 
     phase("turn1")
     await_bytes(tok.at[1], rsem.at[5])
@@ -286,8 +287,31 @@
             dr[pl.ds(i * ts + j * tile, tile), :] = (
                 p[i, at, :] * to_ring * (v - center_dev)
             ).astype(BF16)
+    far = pl.ds(1, n - 1)
+    await_bytes(ph.at[far, pl.ds(0, n // nx)], rsem.at[9])
+    for k in far_first(nx):
+        send(ph.at[far, part], ph.at[far, part], ssem.at[28], rsem.at[26], along_x(k, c))
     phase("a_send")
     chip_sums(a_visit)
+
+    phase("pair_send")
+    pko[0] = jnp.concatenate([peak, peak, blank], axis=0)
+    send(pko.at[0], pko.at[1], ssem.at[23], rsem.at[21], partner)
+    send(p.at[1], po, ssem.at[24], rsem.at[22], partner)
+    send(wg.at[1], wo, ssem.at[25], rsem.at[23], partner)
+    send(w.at[pl.ds(0, sl)], w.at[pl.ds(2 * sl, sl)], ssem.at[26], rsem.at[24], partner)
+
+    def phi_rows():
+        phase("phi_wait")
+        await_bytes(ph.at[far, pl.ds(0, n - n // nx)], rsem.at[26])
+        for i in range(n):
+            for j in range(n):
+                at = ph.at[lax.rem(i * other + j * c + n - a, n), j * other + i * c]
+                phim[(i * n + j) * rows : (i * n + j + 1) * rows] = at[...].astype(F32).reshape(rows, sl)
+        w[sl : 2 * sl, :] = phim[...].T.astype(BF16)
+        send(
+            w.at[pl.ds(sl, sl)], w.at[pl.ds(3 * sl, sl)], ssem.at[27], rsem.at[25], partner
+        )
 
     phase("b_wait")
     at_b = (y, z)
@@ -304,10 +328,6 @@
 
     @pl.when(c == 1)
     def _():
-        await_bytes(brcv.at[0], rsem.at[10])
-        await_bytes(brcv.at[1], rsem.at[11])
-        for h in range(2):
-            spread(h, 0, sum(brcv[h, i].astype(F32) for i in range(n)))
         phase("m_wait")
         await_bytes(st_m.at[0], rsem.at[14])
         await_bytes(st_m.at[1, pl.ds(0, n - 1)], rsem.at[15])
@@ -318,6 +338,10 @@
             for k in order:
                 spot = st_b.at[h, at_b[h]]
                 send(spot, spot, ssem.at[19], rsem.at[16], to_b[h](k, 1))
+        await_bytes(brcv.at[0], rsem.at[10])
+        await_bytes(brcv.at[1], rsem.at[11])
+        for h in range(2):
+            spread(h, 0, sum(brcv[h, i].astype(F32) for i in range(n)))
         for h in range(2):
             low = jnp.zeros((blk, sl), F32)
             for i in range(n):
@@ -332,6 +356,7 @@
             for i in range(n):
                 res = res + arcv[h, i].astype(F32)
             spread(h, 1, res)
+        phi_rows()
         phase("centers")
         await_bytes(st_b.at[:, pl.ds(0, n - 1)], rsem.at[16])
         for h in range(2):
@@ -342,45 +367,37 @@
                 sum(st_b[h, i, q : q + 1] * s for i, s in enumerate(scales)) for q in (0, 1, 3)
             )
             fin_out[h] = jnp.concatenate([dot_sum / weight, top, norm, blank[:1]], axis=0)
-        send(fin_out.at[0], fin, ssem.at[20], rsem.at[19], partner)
-        fin[...] = fin_out[1]
+        send(fin_out, fin, ssem.at[20], rsem.at[19], partner)
+        fin[...] = fin_out[...]
 
     @pl.when(c == 0)
     def _():
+        phi_rows()
+        phase("fin_wait")
         await_bytes(fin, rsem.at[19])
 
-    phase("settle")
-    center = fin[0:1]
-    dev_scale = jnp.exp(peak - fin[1:2]) / fin[2:3]
-    for i in range(2):
-
-        def settle(j, carry, i=i):
-            at = pl.ds(pl.multiple_of(j * tile, tile), tile)
-            dispatch = p[i, at, :] * dev_scale
-            u[i, at, 0:sl] = dispatch.astype(BF16)
-            u[i, at, sl : 2 * sl] = (dispatch * (wg[i, at, :] - center)).astype(BF16)
-            return carry
-
-        lax.fori_loop(0, ts // tile, settle, 0)
-
-    phase("phi_wait")
-    await_bytes(ph.at[pl.ds(0, n - 1)], rsem.at[9])
-    for i in range(n):
-        for j in range(n):
-            at = ph.at[i * other + j * c, j * other + i * c]
-            phim[(i * n + j) * rows : (i * n + j + 1) * rows] = at[...].astype(F32).reshape(rows, sl)
-    w[sl : 2 * sl, :] = phim[...].T.astype(BF16)
-    phase("emit_other")
+    phase("pair_wait")
+    await_bytes(pko.at[1], rsem.at[21])
+    await_bytes(po, rsem.at[22])
+    await_bytes(wo, rsem.at[23])
+    await_bytes(w.at[pl.ds(0, sl)], rsem.at[24])
+    await_bytes(w.at[pl.ds(0, sl)], rsem.at[25])
+    phase("emit")
     grad_scale = float(ts * n * n * 2 // 16)
-
-    def emit_other(j, carry):
-        at = pl.ds(pl.multiple_of(j * tile, tile), tile)
-        s = jnp.dot(u[1, at, :], w[...], preferred_element_type=F32)
-        tgs[at, :] = s.astype(BF16)
-        send(tgs.at[at], tgr.at[at], osem.at[0], osem.at[1 + j], partner)
-        return carry
-
-    lax.fori_loop(0, ts // tile, emit_other, 0)
+    halves = []
+    for q, core in enumerate((c, other)):
+        last = fin[core]
+        scale = jnp.exp(pko[q, 0:1] - last[1:2]) / last[2:3]
+        halves.append((last[0:1], scale))
+    for j in range(ts // tile):
+        at = pl.ds(j * tile, tile)
+        for q, (pv, wv) in enumerate(((p[0, at, :], wg[0, at, :]), (po[at, :], wo[at, :]))):
+            center, scale = halves[q]
+            dispatch = pv * scale
+            u[at, 2 * q * sl : (2 * q + 1) * sl] = dispatch.astype(BF16)
+            u[at, (2 * q + 1) * sl : (2 * q + 2) * sl] = (dispatch * (wv - center)).astype(BF16)
+        s = jnp.dot(u[at, :], w[...], preferred_element_type=F32)
+        tg_o[at, :] = (grad_scale * s).astype(BF16)
 
     phase("r_wait")
 
@@ -400,17 +417,6 @@
         send(xs.at[0], xbuf.at[x], ssem.at[16], rsem.at[20], partner)
         xbuf[x] = xs[1]
 
-    phase("emit_own")
-
-    def emit_own(j, carry):
-        at = pl.ds(pl.multiple_of(j * tile, tile), tile)
-        s = jnp.dot(u[0, at, :], w[...], preferred_element_type=F32)
-        await_bytes(tgr.at[at], osem.at[1 + j])
-        tg_o[at, :] = (grad_scale * (s + tgr[at, :].astype(F32))).astype(BF16)
-        return carry
-
-    lax.fori_loop(0, ts // tile, emit_own, 0)
-
     phase("x_wait")
     @pl.when(c == 0)
     def _():
@@ -434,11 +440,16 @@
     await_bytes(ph.at[0, :, 0], ssem.at[4])
     await_bytes(tok.at[1], ssem.at[5])
     await_bytes(st_a.at[pl.ds(0, n - 1)], ssem.at[6])
-    await_bytes(ph.at[pl.ds(0, n - 1)], ssem.at[9])
+    await_bytes(ph.at[far, pl.ds(0, n // nx)], ssem.at[9])
+    await_bytes(ph.at[far, pl.ds(0, n - n // nx)], ssem.at[28])
     await_bytes(brcv.at[0, pl.ds(0, n - 1)], ssem.at[10])
     await_bytes(st_m.at[0, pl.ds(0, n - 1)], ssem.at[11])
     await_bytes(arcv.at[0, pl.ds(0, n - 1)], ssem.at[13])
-    await_bytes(tgs, osem.at[0])
+    await_bytes(pko.at[0], ssem.at[23])
+    await_bytes(po, ssem.at[24])
+    await_bytes(wo, ssem.at[25])
+    await_bytes(w.at[pl.ds(0, sl)], ssem.at[26])
+    await_bytes(w.at[pl.ds(0, sl)], ssem.at[27])
 
     @pl.when((c == 0) & (near == 1))
     def _():
@@ -489,19 +500,19 @@
     scratch = [
         vm((2, ts, d), BF16), vm((d, 2 * ts), BF16), vm((2, ts, sl), BF16),
         vm((2, ts, sl), F32), vm((2, ts, sl), F32), vm((2 * ts, sl), BF16),
-        vm((2, ts, 2 * sl), BF16), vm((2 * sl, d), BF16), vm((d, sl), F32),
+        vm((ts, 4 * sl), BF16), vm((4 * sl, d), BF16), vm((d, sl), F32),
         vm((gs, half), BF16), vm((rows // 2, sl), BF16),
         vm((n, 2, gs, half), BF16), vm((2, n // 2, n, 2, gs, half), BF16),
         vm((n, n, 2, rows // 2, sl), BF16),
         vm((n, 4, sl), F32), vm((2, n, 4, sl), F32), vm((2, n, 4, sl), F32),
-        vm((2, 4, sl), F32), vm((4, sl), F32),
+        vm((2, 4, sl), F32), vm((2, 4, sl), F32),
         vm((n, n * rows, sl), BF16), vm((2, n, n * rows, sl), BF16),
         vm((n, n * rows, sl), BF16), vm((2, n, n * rows, sl), BF16),
         vm((2, n * rows, sl), F32), vm((d, 2 * sl), BF16),
         vm((2, 2, n, rows, sl), F32), vm((2, 2, n, rows, sl), F32),
         vm((2, rows // 2, 2 * sl), F32), vm((nx, rows // 2, 2 * sl), F32),
-        vm((ts, d), BF16), vm((ts, d), BF16),
-        dma((6,)), dma((23,)), dma((21,)), dma((n // 2,)), dma((1 + ts // tile,)),
+        vm((ts, sl), F32), vm((ts, sl), F32), vm((2, 4, sl), F32),
+        dma((6,)), dma((29,)), dma((27,)), dma((n // 2,)),
     ]
     vm_spec = pl.BlockSpec(memory_space=pltpu.VMEM)
     token_grad, phi_grad = pl.pallas_call(

time: 45.5 us -> 44.6 us (0.980)
  Pallas kernels: 44.8 us -> 43.8 us
    pallas_call x1, Pallas kernels: 43.4 us -> 42.4 us  [per_device(): pl.pallas_call(functools.partial(kernel, n, nx), out_shape=(pltpu.VMEM((t...]
where the time goes in v4:
time: 44.6 us; the launch traced here: 44.5 us
  Pallas kernels  43.8 us (98%)
  between operations  0.64 us (1%)
    pallas_call x1, Pallas kernels, per_device(): pl.pallas_call(functools.partial(kernel, n, nx), out_shape=(pltpu.VMEM((t...  42.4 us
    pallas_call x1, Pallas kernels, per_device(): pl.pallas_call(write_out, out_shape=(jax.ShapeDtypeStruct((ts, d), BF16),...  1.39 us

profile of v4, /device:TPU:1, one launch (start us, length us, event | category | flops | bytes accessed | tf_op | source)
XLA Modules:
  0.0 44.5 jit_solution(10699612349090231562)
XLA Ops:
  0.6 42.4 %moe_dispatch_backward.1 = (bf16[1024,1024]{1,0:T(8,128)(2,1)S(1)}, f32[8,256]{1,0:T(8,128)S(1)}) custom-call(bf16[1024,1024]{1,0:T(8,128)(2,1)} %bitcast.4, bf16[1024,256]{1,0:T(8,128)(2,1)} %bitcast.5, bf16[2,1024]{1,0:T(2,128)(2,1)} %bitcast.6, bf16[8,256]{1,0:T(8,128)(2,1)} %phi_h.1), custom_call_target="tpu_custom_call" | custom-call | tf_op jit(solution)/shard_map/moe_dispatch_backward/pallas_call | solution.py:518
  43.1 1.4 %write_out.1 = (bf16[1024,1024]{1,0:T(8,128)(2,1)}, f32[8,256]{1,0:T(8,128)}) custom-call(bf16[1024,1024]{1,0:T(8,128)(2,1)S(1)} %get-tuple-element.6.tg_v, f32[8,256]{1,0:T(8,128)S(1)} %get-tuple-element.7.pg_v), custom_call_target="tpu_custom_call" | custom-call | tf_op jit(solution)/shard_map/write_out/pallas_call | solution.py:529
